TPU v7x, 512 devices: a whole 4x4x16 slice. The times are simulated.
512 devices in a mesh: row: 32 (over x_lo, z), col: 16 (over x_hi, y, core).
Axes of the slice: x: 4 (x_hi: 2, x_lo: 2; x = x_hi * 2 + x_lo), y: 4, z: 16, core: 2. Of those that a mesh axis runs over, the one named last changes fastest.
Arguments:
- tokens: bfloat16 [256, 12288], P('row', 'col'), may hold values from -6 to 6
- past_tokens: bfloat16 [256, 12288], P('row', 'col'), may hold values from -6 to 6
- out_grad: bfloat16 [256, 12288], P('row', 'col'), may hold values from -3 to 3
- w_in: bfloat16 [12288, 24576], P('col', 'row'), may hold values from -0.0546875 to 0.0546875
- w_out: bfloat16 [24576, 12288], P('row', 'col'), may hold values from -0.0390625 to 0.0390625
Outputs:
- layer_out: bfloat16 [256, 12288], P('row', 'col')
- input_grad: bfloat16 [256, 12288], P('row', 'col')
- grad_w_in: bfloat16 [12288, 24576], P('col', 'row')
- grad_w_out: bfloat16 [24576, 12288], P('row', 'col')
All inputs are finite; a program needn't handle non-finite values.
Results may differ from a plain program's by a relative error of at most 0.005.
Values may be sent and summed in bfloat16 or wider, within the bound.
A program may use at most 64 MiB of HBM per device.

v0:
```python
import jax
import jax.numpy as jnp
from jax import lax
from jax.sharding import Mesh
from jax.sharding import PartitionSpec as P

ROW = ("row_0", "row_1")


def in_order(pieces, dim):
    pieces = jnp.moveaxis(pieces, 0, dim)
    shape = pieces.shape
    return pieces.reshape(*shape[:dim], shape[dim] * shape[dim + 1], *shape[dim + 2 :])


def stacked_from(shard, axes, order):
    pieces = shard[None]
    for k in order:
        pieces = lax.all_gather(pieces, axes[k], axis=0, tiled=True)
    carried = [lax.axis_size(axes[k]) for k in reversed(order)]
    pieces = pieces.reshape(*carried, *shard.shape)
    turned = sorted(range(len(order)), key=lambda place: order[len(order) - 1 - place])
    return pieces.transpose(*turned, *range(len(order), pieces.ndim)).reshape(-1, *shard.shape)


def gather_axes(shard, axes, order, dim):
    return in_order(stacked_from(shard, axes, order), dim)


def cut_along(shard, dim, length):
    shape = shard.shape
    pieces = shard.reshape(*shape[:dim], length, shape[dim] // length, *shape[dim + 1 :])
    return jnp.moveaxis(pieces, dim, 0)


def sent_and_summed(shard, axis, dim):
    pieces = cut_along(shard, dim, lax.axis_size(axis))
    arrived = lax.all_to_all(pieces, axis, split_axis=0, concat_axis=0, tiled=True)
    return arrived.sum(axis=0)


def sent_to_all(shard, axis):
    copies = jnp.broadcast_to(shard, (lax.axis_size(axis), *shard.shape))
    return lax.all_to_all(copies, axis, split_axis=0, concat_axis=0, tiled=True)


def gathered_copies(shard, axis, dim):
    return in_order(sent_to_all(shard, axis), dim)


def sent_together(arrays, axis, dim, along):
    both = jnp.concatenate(arrays, axis=along)
    out, at, gathered = (lax.all_gather(both, axis, axis=dim, tiled=True), 0, [])
    for a in arrays:
        gathered.append(lax.slice_in_dim(out, at, at + a.shape[along], axis=along))
        at += a.shape[along]
    return tuple(gathered)


def in_one_piece(arrays, axis, dim, along):
    widths = [a.shape[along] for a in arrays]
    both = jnp.concatenate(arrays, axis=along)
    out = lax.psum_scatter(both, axis, scatter_dimension=dim, tiled=True)
    return tuple(jnp.split(out, [sum(widths[:k]) for k in range(1, len(widths))], axis=along))


def gelu_parts(pre):
    cdf = 0.5 * (1.0 + jax.scipy.special.erf(pre * 0.7071067811865476))
    slope = cdf + pre * jnp.exp(-0.5 * pre * pre) * 0.3989422804014327
    return (pre * cdf, slope)


def local(tokens, past_tokens, out_grad, w_in, w_out):
    pre_part = jnp.dot(
        gather_axes(tokens, ROW, (0, 1), 0), w_in, preferred_element_type=jnp.float32
    )
    pre_share = sent_and_summed(pre_part, "col", 0)
    hidden_share = gelu_parts(pre_share)[0].astype(jnp.bfloat16)
    hidden_all = gathered_copies(hidden_share, "col", 0)
    block = hidden_all
    layer_out = sent_and_summed(
        jnp.dot(block, w_out, preferred_element_type=jnp.float32), ROW, 0
    ).astype(jnp.bfloat16)
    past_all, grad_all = sent_together((past_tokens, out_grad), ROW, 0, 1)
    past_part = jnp.dot(past_all, w_in, preferred_element_type=jnp.float32)
    back_part = lax.dot_general(
        grad_all, w_out, (((1,), (1,)), ((), ())), preferred_element_type=jnp.float32
    )
    past_share, back_share = in_one_piece((past_part, back_part), "col", 0, 1)
    act_share, slope = gelu_parts(past_share)
    act_local = act_share.astype(jnp.bfloat16)
    grad_local = (back_share * slope).astype(jnp.bfloat16)
    act_all, hidden_grad = sent_together((act_local, grad_local), "col", 0, 1)
    grad_w_out = lax.dot_general(
        act_all, grad_all, (((0,), (0,)), ((), ())), preferred_element_type=jnp.float32
    ).astype(jnp.bfloat16)
    grad_w_in = lax.dot_general(
        past_all, hidden_grad, (((0,), (0,)), ((), ())), preferred_element_type=jnp.float32
    ).astype(jnp.bfloat16)
    block = hidden_grad
    input_grad = sent_and_summed(
        lax.dot_general(block, w_in, (((1,), (1,)), ((), ())), preferred_element_type=jnp.float32),
        ROW,
        0,
    ).astype(jnp.bfloat16)
    return (layer_out, input_grad, grad_w_in, grad_w_out)


def solution(mesh):
    split = Mesh(mesh.devices.reshape(2, 16, mesh.shape["col"]), ("row_0", "row_1", "col"))
    return jax.shard_map(
        local,
        mesh=split,
        in_specs=(P(ROW, "col"), P(ROW, "col"), P(ROW, "col"), P("col", ROW), P(ROW, "col")),
        out_specs=(P(ROW, "col"), P(ROW, "col"), P("col", ROW), P(ROW, "col")),
        check_vma=False,
    )
```

profile of v0, /device:TPU:32, one launch (start us, length us, event | category | flops | bytes accessed | tf_op | source)
XLA Modules:
  0.0 314.2 jit_solution(4100335702246159757)
XLA Ops:
  7.2 0.0 copy-start
  7.2 4.7 %all-gather = bf16[16,768]{1,0:T(8,128)(2,1)S(1)} all-gather(bf16[8,768]{1,0:T(8,128)(2,1)} %param.5), channel_id=2, replica_groups=mesh['row_0'=2,'row_1'=16,'col'=16] {'row_0'}, dimensions={0}, use_global_device_ids=true | all-gather | bytes 36864 | tf_op jit(solution)/shard_map/all_gather | solution.py:19
  11.9 35.8 %all_gather.13 = bf16[32,8,768]{2,1,0:T(8,128)(2,1)S(1)} all-gather(bf16[2,8,768]{2,1,0:T(8,128)(2,1)S(1)} %bitcast.22), channel_id=1, replica_groups=mesh['row_0'=2,'row_1'=16,'col'=16] {'row_1'}, dimensions={0}, use_global_device_ids=true | all-gather | bytes 417792 | tf_op jit(solution)/shard_map/all_gather | solution.py:19
  47.8 0.0 copy-done
  47.8 1.4 fusion.2
  49.1 0.0 copy-start.3
  49.1 0.0 copy-start.4
  49.1 7.2 %all-to-all-start = ((f32[16,16,768]{2,1,0:T(8,128)}), f32[16,16,768]{2,1,0:T(8,128)}, u32[]{:S(2)}, u32[]{:S(2)}) async-start(f32[16,16,768]{2,1,0:T(8,128)} %fusion.2), calls=%async_computation | async-start | bytes 1572864 | tf_op jit(solution)/shard_map/all_to_all | solution.py:38
  56.4 0.0 copy-done.3
  56.4 0.0 copy-done.4
  56.4 64.7 %all_gather.14 = bf16[256,1536]{1,0:T(8,128)(2,1)S(1)} all-gather(bf16[8,1536]{1,0:T(8,128)(2,1)S(1)} %pad_maximum_fusion.2), channel_id=1, replica_groups=mesh['row_0'=2,'row_1'=16,'col'=16] {'row_0','row_1'}, dimensions={0}, use_global_device_ids=true | all-gather | bytes 811008 | tf_op jit(solution)/shard_map/all_gather | solution.py:53
  121.1 1.4 fusion.11
  122.4 0.0 copy-start.1
  122.4 0.0 all-to-all-done
  122.4 1.3 reduce_sum.27
  123.8 0.8 broadcast_in_dim.7
  124.5 7.2 %all-to-all-start.1 = ((bf16[16,16,768]{2,1,0:T(8,128)(2,1)}), bf16[16,16,768]{2,1,0:T(8,128)(2,1)S(1)}, u32[]{:S(2)}, u32[]{:S(2)}) async-start(bf16[16,16,768]{2,1,0:T(8,128)(2,1)} %broadcast_in_dim.7), calls=%async_computation.1 | async-start | bytes 786432 | tf_op jit(solution)/shard_map/all_to_all | solution.py:44
  131.8 0.0 reduce-scatter.2.cloned.1.call-start
  131.8 0.0 copy-done.1
  131.8 0.0 copy-start.2
  131.9 0.5 fusion.8
  132.4 0.6 copy-done.2
  133.0 1.3 pad_maximum_fusion
  134.3 0.0 reduce-scatter.2.cloned.1.call-update
  134.3 8.4 %all-to-all-done.1 = bf16[16,16,768]{2,1,0:T(8,128)(2,1)S(1)} async-done(((bf16[16,16,768]{2,1,0:T(8,128)(2,1)}), bf16[16,16,768]{2,1,0:T(8,128)(2,1)S(1)}, u32[]{:S(2)}, u32[]{:S(2)}) %all-to-all-start.1) | async-done | bytes 393248 | tf_op jit(solution)/shard_map/all_to_all | solution.py:44
  142.7 1.4 fusion
  144.1 4.4 %all-to-all-start.2 = ((f32[32,8,768]{2,1,0:T(8,128)}), f32[32,8,768]{2,1,0:T(8,128)S(1)}, u32[]{:S(2)}, u32[]{:S(2)}) async-start(f32[32,8,768]{2,1,0:T(8,128)} %fusion), calls=%async_computation.2 | async-start | bytes 1572864 | tf_op jit(solution)/shard_map/all_to_all | solution.py:38
  148.5 73.4 %reduce-scatter.2.cloned.1.call-done = f32[16,1536]{1,0:T(8,128)} async-done(((f32[256,1536]{1,0:T(8,128)}), f32[16,1536]{1,0:T(8,128)}) %reduce-scatter.2.cloned.1.call-update) | async-done | bytes 98320 | tf_op jit(solution)/shard_map/reduce_scatter | solution.py:63
  221.8 0.9 multiply_convert_fusion
  222.7 23.7 %all_gather.15 = bf16[256,1536]{1,0:T(8,128)(2,1)S(1)} all-gather(bf16[16,1536]{1,0:T(8,128)(2,1)S(1)} %pad_maximum_fusion.1), channel_id=1, replica_groups=mesh['row_0'=2,'row_1'=16,'col'=16] {'col'}, dimensions={0}, use_global_device_ids=true | all-gather | bytes 835584 | tf_op jit(solution)/shard_map/all_gather | solution.py:53
  246.4 1.4 convolution_bitcast_fusion
  247.8 0.0 all-to-all-done.2
  247.8 13.6 %all-to-all-start.3 = ((f32[32,8,768]{2,1,0:T(8,128)}), f32[32,8,768]{2,1,0:T(8,128)}, u32[]{:S(2)}, u32[]{:S(2)}) async-start(f32[32,8,768]{2,1,0:T(8,128)} %convolution_bitcast_fusion), calls=%async_computation.4 | async-start | bytes 1572864 | tf_op jit(solution)/shard_map/all_to_all | solution.py:38
  261.4 1.5 convolution_convert_fusion
  263.0 1.5 convolution_convert_fusion.1
  264.5 0.7 reduce_sum.28
  265.1 40.4 %all-to-all-done.3 = f32[32,8,768]{2,1,0:T(8,128)} async-done(((f32[32,8,768]{2,1,0:T(8,128)}), f32[32,8,768]{2,1,0:T(8,128)}, u32[]{:S(2)}, u32[]{:S(2)}) %all-to-all-start.3) | async-done | bytes 786464 | tf_op jit(solution)/shard_map/all_to_all | solution.py:38
  305.6 1.8 reduce_sum.29
  (4 shorter events, 0.1 us)
Async XLA Ops:
  7.2 40.6 %copy-start = (bf16[768,768]{1,0:T(8,128)(2,1)S(1)}, bf16[768,768]{1,0:T(8,128)(2,1)}, u32[]{:S(2)}) copy-start(bf16[768,768]{1,0:T(8,128)(2,1)} %param.8) | copy-start | bytes 3538948
  49.1 7.2 %copy-start.3 = (bf16[8,768]{1,0:T(8,128)(2,1)S(1)}, bf16[8,768]{1,0:T(8,128)(2,1)}, u32[]{:S(2)}) copy-start(bf16[8,768]{1,0:T(8,128)(2,1)} %param.7) | copy-start | bytes 36868
  49.1 7.2 %copy-start.4 = (bf16[8,768]{1,0:T(8,128)(2,1)S(1)}, bf16[8,768]{1,0:T(8,128)(2,1)}, u32[]{:S(2)}) copy-start(bf16[8,768]{1,0:T(8,128)(2,1)} %param.6) | copy-start | bytes 36868
  49.1 73.3 %all-to-all-start = ((f32[16,16,768]{2,1,0:T(8,128)}), f32[16,16,768]{2,1,0:T(8,128)}, u32[]{:S(2)}, u32[]{:S(2)}) async-start(f32[16,16,768]{2,1,0:T(8,128)} %fusion.2), calls=%async_computation | async-start | bytes 1572864 | tf_op jit(solution)/shard_map/all_to_all | solution.py:38
  122.4 9.4 %copy-start.1 = (bf16[768,768]{1,0:T(8,128)(2,1)S(1)}, bf16[768,768]{1,0:T(8,128)(2,1)}, u32[]{:S(2)}) copy-start(bf16[768,768]{1,0:T(8,128)(2,1)} %param.9) | copy-start | bytes 3538948
  124.5 18.2 %all-to-all-start.1 = ((bf16[16,16,768]{2,1,0:T(8,128)(2,1)}), bf16[16,16,768]{2,1,0:T(8,128)(2,1)S(1)}, u32[]{:S(2)}, u32[]{:S(2)}) async-start(bf16[16,16,768]{2,1,0:T(8,128)(2,1)} %broadcast_in_dim.7), calls=%async_computation.1 | async-start | bytes 786432 | tf_op jit(solution)/shard_map/all_to_all | solution.py:44
  131.8 90.1 %reduce-scatter.2.cloned.1.call-start = ((), (), s32[]{:S(2)}) async-start(), calls=%async_computation.5 | async-start | bytes 1671168 | tf_op jit(solution)/shard_map/reduce_scatter | solution.py:63
  131.8 1.1 copy-start.2
  144.1 103.7 %all-to-all-start.2 = ((f32[32,8,768]{2,1,0:T(8,128)}), f32[32,8,768]{2,1,0:T(8,128)S(1)}, u32[]{:S(2)}, u32[]{:S(2)}) async-start(f32[32,8,768]{2,1,0:T(8,128)} %fusion), calls=%async_computation.2 | async-start | bytes 1572864 | tf_op jit(solution)/shard_map/all_to_all | solution.py:38
  247.8 57.8 %all-to-all-start.3 = ((f32[32,8,768]{2,1,0:T(8,128)}), f32[32,8,768]{2,1,0:T(8,128)}, u32[]{:S(2)}, u32[]{:S(2)}) async-start(f32[32,8,768]{2,1,0:T(8,128)} %convolution_bitcast_fusion), calls=%async_computation.4 | async-start | bytes 1572864 | tf_op jit(solution)/shard_map/all_to_all | solution.py:38
Sparse Core Ops, SparseCore 0:
  137.4 84.4 reduce-scatter.1
where the time goes:
time: 315 us; the launch traced here: 314 us
  blocking collectives  129 us (41%)
  waiting for transfers between devices  122 us (39%)
  starting transfers between devices  32.5 us (10%)
  between operations  14.2 us (5%)
  matrix products  9.03 us (3%)
  other arithmetic  5.96 us (2%)
    all_gather x2, blocking collectives, sent_together(): lax.all_gather(both, axis, axis=dim, tiled=True)  88.3 us
    reduce_scatter x1, waiting for transfers between devices, in_one_piece(): out = lax.psum_scatter(both, axis, scatter_dimension=dim, tiled=True)  73.4 us
    all_gather x2, blocking collectives, stacked_from(): pieces = lax.all_gather(pieces, axes[k], axis=0, tiled=True)  40.6 us
    all_to_all x3, waiting for transfers between devices, sent_and_summed(): lax.all_to_all(pieces, axis, split_axis=0, concat_axis=0, tiled=True)  40.4 us
    all_to_all x3, starting transfers between devices, sent_and_summed(): lax.all_to_all(pieces, axis, split_axis=0, concat_axis=0, tiled=True)  25.3 us
    all_to_all x1, waiting for transfers between devices, sent_to_all(): return lax.all_to_all(copies, axis, split_axis=0, concat_axis=0, tiled=True)  8.37 us
    all_to_all x1, starting transfers between devices, sent_to_all(): return lax.all_to_all(copies, axis, split_axis=0, concat_axis=0, tiled=True)  7.25 us
  transfers between devices with their start and end apart: 5, of which 3 were waited for; matrix products, arithmetic and copies ran while one was open for 3% of the time, Pallas kernels for 0%

commit v1 on v0

--- a/solution.py
+++ b/solution.py
@@ -16,7 +16,16 @@
 def stacked_from(shard, axes, order):
     pieces = shard[None]
     for k in order:
-        pieces = lax.all_gather(pieces, axes[k], axis=0, tiled=True)
+        frame = axes[k]
+        pieces = jnp.concatenate(
+            lax.all_to_all(
+                jnp.stack([pieces for _ in range(lax.axis_size(frame))]),
+                axis_name=frame,
+                split_axis=0,
+                concat_axis=0,
+            ),
+            0,
+        )
     carried = [lax.axis_size(axes[k]) for k in reversed(order)]
     pieces = pieces.reshape(*carried, *shard.shape)
     turned = sorted(range(len(order)), key=lambda place: order[len(order) - 1 - place])

time: 315 us -> 336 us (1.067)
  waiting for transfers between devices: 122 us -> 150 us
  blocking collectives: 129 us -> 117 us
    all_gather x2 -> x0, blocking collectives: 40.6 us -> none  [stacked_from(): pieces = lax.all_gather(pieces, axes[k], axis=0, tiled=True)]
    all_to_all x3 -> x2, waiting for transfers between devices: 40.4 us -> 80.8 us  [sent_and_summed(): lax.all_to_all(pieces, axis, split_axis=0, concat_axis=0, tiled=True)]
    all_to_all x0 -> x1, blocking collectives: none -> 22 us  [sent_and_summed(): lax.all_to_all(pieces, axis, split_axis=0, concat_axis=0, tiled=True)]
    reduce_scatter x1, waiting for transfers between devices: 73.4 us -> 54.7 us  [in_one_piece(): out = lax.psum_scatter(both, axis, scatter_dimension=dim, tiled=True)]
    all_to_all x0 -> x2, waiting for transfers between devices: none -> 14.4 us  [stacked_from(): lax.all_to_all(jnp.stack([pieces for _ in range(lax.axis_size(frame))]),...]
    all_to_all x0 -> x2, starting transfers between devices: none -> 12.7 us  [stacked_from(): lax.all_to_all(jnp.stack([pieces for _ in range(lax.axis_size(frame))]),...]
    all_to_all x1, waiting for transfers between devices: 8.37 us -> 0.01 us  [sent_to_all(): return lax.all_to_all(copies, axis, split_axis=0, concat_axis=0, tiled=True)]
    all_to_all x3 -> x2, starting transfers between devices: 25.3 us -> 18 us  [sent_and_summed(): lax.all_to_all(pieces, axis, split_axis=0, concat_axis=0, tiled=True)]
  transfers between devices with their start and end apart: 5 -> 6, of which waited for: 3 -> 4; matrix products, arithmetic and copies ran while one was open for 3% -> 4% of each run, Pallas kernels for 0% -> 0%
where the time goes in v1:
time: 336 us; the launch traced here: 335 us
  waiting for transfers between devices  150 us (45%)
  blocking collectives  117 us (35%)
  starting transfers between devices  34.3 us (10%)
  between operations  14.1 us (4%)
  matrix products  9.55 us (3%)
  other arithmetic  6.87 us (2%)
    all_gather x2, blocking collectives, sent_together(): lax.all_gather(both, axis, axis=dim, tiled=True)  95.4 us
    all_to_all x2, waiting for transfers between devices, sent_and_summed(): lax.all_to_all(pieces, axis, split_axis=0, concat_axis=0, tiled=True)  80.8 us
    reduce_scatter x1, waiting for transfers between devices, in_one_piece(): out = lax.psum_scatter(both, axis, scatter_dimension=dim, tiled=True)  54.7 us
    all_to_all x1, blocking collectives, sent_and_summed(): lax.all_to_all(pieces, axis, split_axis=0, concat_axis=0, tiled=True)  22 us
    all_to_all x2, starting transfers between devices, sent_and_summed(): lax.all_to_all(pieces, axis, split_axis=0, concat_axis=0, tiled=True)  18 us
    all_to_all x2, waiting for transfers between devices, stacked_from(): lax.all_to_all(jnp.stack([pieces for _ in range(lax.axis_size(frame))]),...  14.4 us
    all_to_all x2, starting transfers between devices, stacked_from(): lax.all_to_all(jnp.stack([pieces for _ in range(lax.axis_size(frame))]),...  12.7 us
  transfers between devices with their start and end apart: 6, of which 4 were waited for; matrix products, arithmetic and copies ran while one was open for 4% of the time, Pallas kernels for 0%

profile of v1, /device:TPU:32, one launch (start us, length us, event | category | flops | bytes accessed | tf_op | source)
XLA Modules:
  0.0 335.2 jit_solution(10996247170398883568)
XLA Ops:
  7.2 0.0 copy-start
  7.2 1.4 pad_maximum_fusion.2
  8.6 3.2 all-to-all-start
  11.9 0.7 pad_maximum_fusion.3
  12.6 71.7 %all_gather.6 = bf16[256,1536]{1,0:T(8,128)(2,1)S(1)} all-gather(bf16[8,1536]{1,0:T(8,128)(2,1)S(1)} %pad_maximum_fusion.3), channel_id=1, replica_groups=mesh['row_0'=2,'row_1'=16,'col'=16] {'row_0','row_1'}, dimensions={0}, use_global_device_ids=true | all-gather | bytes 811008 | tf_op jit(solution)/shard_map/all_gather | solution.py:62
  84.3 0.0 copy-done
  84.3 1.4 fusion.11
  85.6 0.0 copy-start.1
  85.6 0.0 all-to-all-done
  85.7 0.8 stack.7
  86.4 9.5 %all-to-all-start.1 = ((bf16[16,2,8,768]{3,2,1,0:T(8,128)(2,1)}), bf16[16,2,8,768]{3,2,1,0:T(8,128)(2,1)S(1)}, u32[]{:S(2)}, u32[]{:S(2)}) async-start(bf16[16,2,8,768]{3,2,1,0:T(8,128)(2,1)} %stack.7), calls=%async_computation.1 | async-start | bytes 786432 | tf_op jit(solution)/shard_map/all_to_all | solution.py:21
  95.9 0.0 reduce-scatter.2.cloned.1.call-start
  95.9 0.0 copy-done.1
  95.9 0.0 copy-start.2
  96.0 0.5 fusion.8
  96.5 0.6 copy-done.2
  97.1 1.3 pad_maximum_fusion
  98.4 0.0 reduce-scatter.2.cloned.1.call-update
  98.4 14.4 %all-to-all-done.1 = bf16[16,2,8,768]{3,2,1,0:T(8,128)(2,1)S(1)} async-done(((bf16[16,2,8,768]{3,2,1,0:T(8,128)(2,1)}), bf16[16,2,8,768]{3,2,1,0:T(8,128)(2,1)S(1)}, u32[]{:S(2)}, u32[]{:S(2)}) %all-to-all-start.1) | async-done | bytes 393248 | tf_op jit(solution)/shard_map/all_to_all | solution.py:21
  112.9 0.5 fusion.2
  113.4 22.0 %all_to_all.30 = f32[16,16,768]{2,1,0:T(8,128)S(1)} all-to-all(f32[16,16,768]{2,1,0:T(8,128)S(1)} %fusion.2), channel_id=1, replica_groups=mesh['row_0'=2,'row_1'=16,'col'=16] {'col'}, dimensions={0} | all-to-all | bytes 1572864 | tf_op jit(solution)/shard_map/all_to_all | solution.py:47
  135.4 0.8 broadcast_in_dim.3
  136.2 3.6 %all-to-all-start.3 = ((bf16[16,16,768]{2,1,0:T(8,128)(2,1)}), bf16[16,16,768]{2,1,0:T(8,128)(2,1)S(1)}, u32[]{:S(2)}, u32[]{:S(2)}) async-start(bf16[16,16,768]{2,1,0:T(8,128)(2,1)} %broadcast_in_dim.3), calls=%async_computation.3 | async-start | bytes 786432 | tf_op jit(solution)/shard_map/all_to_all | solution.py:53
  139.8 54.7 %reduce-scatter.2.cloned.1.call-done = f32[16,1536]{1,0:T(8,128)} async-done(((f32[256,1536]{1,0:T(8,128)}), f32[16,1536]{1,0:T(8,128)}) %reduce-scatter.2.cloned.1.call-update) | async-done | bytes 98320 | tf_op jit(solution)/shard_map/reduce_scatter | solution.py:72
  194.5 0.9 multiply_convert_fusion
  195.4 23.7 %all_gather.7 = bf16[256,1536]{1,0:T(8,128)(2,1)S(1)} all-gather(bf16[16,1536]{1,0:T(8,128)(2,1)S(1)} %pad_maximum_fusion.1), channel_id=1, replica_groups=mesh['row_0'=2,'row_1'=16,'col'=16] {'col'}, dimensions={0}, use_global_device_ids=true | all-gather | bytes 835584 | tf_op jit(solution)/shard_map/all_gather | solution.py:62
  219.1 1.4 convolution_bitcast_fusion
  220.5 0.0 all-to-all-done.3
  220.5 0.0 copy-start.3
  220.5 0.7 copy-done.3
  221.2 13.6 %all-to-all-start.5 = ((f32[32,8,768]{2,1,0:T(8,128)}), f32[32,8,768]{2,1,0:T(8,128)S(1)}, u32[]{:S(2)}, u32[]{:S(2)}) async-start(f32[32,8,768]{2,1,0:T(8,128)} %convolution_bitcast_fusion), calls=%async_computation.6 | async-start | bytes 1572864 | tf_op jit(solution)/shard_map/all_to_all | solution.py:47
  234.8 2.8 fusion
  237.6 41.3 %all-to-all-done.5 = f32[32,8,768]{2,1,0:T(8,128)S(1)} async-done(((f32[32,8,768]{2,1,0:T(8,128)}), f32[32,8,768]{2,1,0:T(8,128)S(1)}, u32[]{:S(2)}, u32[]{:S(2)}) %all-to-all-start.5) | async-done | bytes 786464 | tf_op jit(solution)/shard_map/all_to_all | solution.py:47
  278.9 4.4 %all-to-all-start.4 = ((f32[32,8,768]{2,1,0:T(8,128)}), f32[32,8,768]{2,1,0:T(8,128)}, u32[]{:S(2)}, u32[]{:S(2)}) async-start(f32[32,8,768]{2,1,0:T(8,128)} %fusion), calls=%async_computation.4 | async-start | bytes 1572864 | tf_op jit(solution)/shard_map/all_to_all | solution.py:47
  283.3 1.5 convolution_convert_fusion
  284.8 1.5 convolution_convert_fusion.1
  286.4 0.7 reduce_sum.29
  287.0 39.5 %all-to-all-done.4 = f32[32,8,768]{2,1,0:T(8,128)} async-done(((f32[32,8,768]{2,1,0:T(8,128)}), f32[32,8,768]{2,1,0:T(8,128)}, u32[]{:S(2)}, u32[]{:S(2)}) %all-to-all-start.4) | async-done | bytes 786464 | tf_op jit(solution)/shard_map/all_to_all | solution.py:47
  326.5 1.8 reduce_sum.28
  (4 shorter events, 0.1 us)
Async XLA Ops:
  7.2 77.1 %copy-start = (bf16[768,768]{1,0:T(8,128)(2,1)S(1)}, bf16[768,768]{1,0:T(8,128)(2,1)}, u32[]{:S(2)}) copy-start(bf16[768,768]{1,0:T(8,128)(2,1)} %param.8) | copy-start | bytes 3538948
  8.6 77.0 %all-to-all-start = ((bf16[2,1,8,768]{3,2,1,0:T(8,128)(2,1)}), bf16[2,1,8,768]{3,2,1,0:T(8,128)(2,1)S(1)}, u32[]{:S(2)}, u32[]{:S(2)}) async-start(bf16[2,1,8,768]{3,2,1,0:T(8,128)(2,1)} %pad_maximum_fusion.2), calls=%async_computation | async-start | bytes 49152 | tf_op jit(solution)/shard_map/all_to_all | solution.py:21
  85.6 10.3 %copy-start.1 = (bf16[768,768]{1,0:T(8,128)(2,1)S(1)}, bf16[768,768]{1,0:T(8,128)(2,1)}, u32[]{:S(2)}) copy-start(bf16[768,768]{1,0:T(8,128)(2,1)} %param.9) | copy-start | bytes 3538948
  86.4 26.5 %all-to-all-start.1 = ((bf16[16,2,8,768]{3,2,1,0:T(8,128)(2,1)}), bf16[16,2,8,768]{3,2,1,0:T(8,128)(2,1)S(1)}, u32[]{:S(2)}, u32[]{:S(2)}) async-start(bf16[16,2,8,768]{3,2,1,0:T(8,128)(2,1)} %stack.7), calls=%async_computation.1 | async-start | bytes 786432 | tf_op jit(solution)/shard_map/all_to_all | solution.py:21
  95.9 98.6 %reduce-scatter.2.cloned.1.call-start = ((), (), s32[]{:S(2)}) async-start(), calls=%async_computation.7 | async-start | bytes 1671168 | tf_op jit(solution)/shard_map/reduce_scatter | solution.py:72
  95.9 1.1 copy-start.2
  136.2 84.2 %all-to-all-start.3 = ((bf16[16,16,768]{2,1,0:T(8,128)(2,1)}), bf16[16,16,768]{2,1,0:T(8,128)(2,1)S(1)}, u32[]{:S(2)}, u32[]{:S(2)}) async-start(bf16[16,16,768]{2,1,0:T(8,128)(2,1)} %broadcast_in_dim.3), calls=%async_computation.3 | async-start | bytes 786432 | tf_op jit(solution)/shard_map/all_to_all | solution.py:53
  220.5 0.7 copy-start.3
  221.2 57.7 %all-to-all-start.5 = ((f32[32,8,768]{2,1,0:T(8,128)}), f32[32,8,768]{2,1,0:T(8,128)S(1)}, u32[]{:S(2)}, u32[]{:S(2)}) async-start(f32[32,8,768]{2,1,0:T(8,128)} %convolution_bitcast_fusion), calls=%async_computation.6 | async-start | bytes 1572864 | tf_op jit(solution)/shard_map/all_to_all | solution.py:47
  278.9 47.7 %all-to-all-start.4 = ((f32[32,8,768]{2,1,0:T(8,128)}), f32[32,8,768]{2,1,0:T(8,128)}, u32[]{:S(2)}, u32[]{:S(2)}) async-start(f32[32,8,768]{2,1,0:T(8,128)} %fusion), calls=%async_computation.4 | async-start | bytes 1572864 | tf_op jit(solution)/shard_map/all_to_all | solution.py:47
Sparse Core Ops, SparseCore 0:
  101.5 92.9 reduce-scatter.1
